TPU v7x, 256 devices: a 4x2x16 block of a 4x16x16 slice. The times are simulated.
256 devices in a mesh: groups: 2 (over y), rows: 16 (over z), sub: 8 (over x, core).
Axes of the slice: x: 4, y: 2, z: 16, core: 2. Of those that a mesh axis runs over, the one named last changes fastest.
The devices are a block of a 4x16x16 slice.
Arguments:
- matrix: float32 [131072, 1024], P(('groups', 'rows', 'sub')), parts along dimension 0
- sign_bits: int32 [131072], P(('groups', 'rows', 'sub')), parts along dimension 0, may hold values from 0 to 1
- samples: int32 [8192], P('groups'), parts along dimension 0, may hold values from 0 to 65535
Outputs:
- cholesky_factor: float32 [2048, 1024], P('groups'), parts along dimension 0
There are 2 independent parts, one for each index of `groups`. A program takes and returns all parts, laid end to end along the dimension named above; each array names one. Nothing has to cross between parts.
Inputs may be any that keep to these rules, and one draw needn't show every extreme that they name: `samples`: row numbers of the whole matrix, drawn independently; a row may be drawn more than once.
All inputs are finite; a program needn't handle non-finite values.
Results may differ from a plain program's by a relative error of at most 0.00011.
Values sent between devices are 32-bit elements; how exact they have to be, the bound alone decides.
A program may use at most 64 MiB of HBM per device.

v0:
```python
import jax
import jax.numpy as jnp
from jax import lax
from jax.sharding import Mesh
from jax.sharding import PartitionSpec as P

ROWS_SUB = ("rows", "sub_0", "sub_1")
GROUPS_ROWS_SUB = ("groups", "rows", "sub_0", "sub_1")


HIGHEST = lax.Precision.HIGHEST


def rows_for(lines, peers):
    spare = -len(lines) % peers
    return jnp.pad(lines, [(0, spare)] + [(0, 0)] * (lines.ndim - 1))


def from_everyone(array, axis):
    peers = lax.axis_size(axis)
    return lax.all_to_all(
        jnp.broadcast_to(array[None], (peers, *array.shape)), axis, 0, 0, tiled=True
    )


def joined_along(pieces, dim):
    dims = list(pieces.shape[1:])
    dims[dim] *= pieces.shape[0]
    return jnp.moveaxis(pieces, 0, dim).reshape(dims)


def gathered_by_axis(array, axes, dim):
    far, near = axes
    first = from_everyone(array, far)
    pieces = jnp.swapaxes(from_everyone(first, near), 0, 1)
    return joined_along(pieces.reshape(-1, *array.shape), dim)


def cut_along(array, dim, peers):
    before, after = (array.shape[:dim], array.shape[dim + 1 :])
    return jnp.moveaxis(array.reshape(*before, peers, -1, *after), dim, 0)


def summed_on_arrival(array, axis, dim):
    peers = lax.axis_size(axis)
    pieces = lax.all_to_all(cut_along(array, dim, peers), axis, 0, 0, tiled=True)
    return jnp.sum(pieces, axis=0)


def sum_by_axis(array, axes, dim):
    far, near = axes
    own = summed_on_arrival(cut_along(array, dim, lax.axis_size(far)), near, dim + 1)
    return jnp.sum(lax.all_to_all(own, far, 0, 0, tiled=True), axis=0)


def nested_sum(array, axes):
    padded = rows_for(array, lax.axis_size(axes[0]) * lax.axis_size(axes[1]))
    whole = gathered_by_axis(sum_by_axis(padded, axes, 0), axes, 0)
    return lax.slice_in_dim(whole, 0, len(array)).reshape(array.shape)


def packed_total(arrays, axis):
    ends = [0]
    for a in arrays:
        ends.append(ends[-1] + a.size)
    total = nested_sum(jnp.concatenate([a.ravel() for a in arrays]), axis)
    return tuple((total[b:e].reshape(a.shape) for a, b, e in zip(arrays, ends, ends[1:])))


def hadamard_table(extent):
    line_ids = jnp.arange(extent, dtype=jnp.int32)
    correlation = jnp.bitwise_and(line_ids[:, None], line_ids[None, :])
    parity = jnp.zeros((extent, extent), jnp.int32)
    for bit_pos in range(extent.bit_length() - 1):
        parity = parity + jnp.bitwise_and(jnp.right_shift(correlation, bit_pos), 1)
    return (1 - 2 * (parity % 2)).astype(jnp.float32)


def local_transform(values):
    rows_here, columns = values.shape
    inner_size = min(rows_here, 128)
    outer_size = rows_here // inner_size
    blocks = values.reshape(outer_size, inner_size, columns)
    blocks = jnp.einsum("ab,qbn->qan", hadamard_table(inner_size), blocks, precision=HIGHEST)
    blocks = jnp.einsum("pq,qan->pan", hadamard_table(outer_size), blocks, precision=HIGHEST)
    return blocks.reshape(rows_here, columns)


def mix_sources(received):
    return jnp.einsum("ab,bjn->ajn", hadamard_table(received.shape[0]), received, precision=HIGHEST)


def body(matrix, sign_bits, samples):
    rows_here, columns = matrix.shape
    devices = lax.axis_size(ROWS_SUB)
    position = lax.axis_index(ROWS_SUB)
    per_block = rows_here // devices
    sign_values = (2 * sign_bits - 1).astype(jnp.float32)
    current = local_transform(matrix * sign_values[:, None])
    block_ids = (
        (jnp.arange(devices, dtype=jnp.int32) * rows_here)[:, None]
        + position * per_block
        + jnp.arange(per_block, dtype=jnp.int32)[None, :]
    )
    blocks = current.reshape(devices, per_block, columns)
    mixed_rows = mix_sources(
        lax.all_to_all(blocks, ROWS_SUB, split_axis=0, concat_axis=0, tiled=True)
    )
    owned_rows = mixed_rows.reshape(rows_here, columns)
    row_ids = block_ids.reshape(rows_here)
    matches = (row_ids[:, None] == samples[None, :]).astype(jnp.float32)
    counts = jnp.sum(matches, axis=1)
    weighted = owned_rows * counts[:, None]
    total_rows = rows_here * devices
    own_terms = jnp.einsum("rn,rm->nm", weighted, owned_rows, precision=HIGHEST) / jnp.float32(
        total_rows * samples.shape[0]
    )
    half_size = columns // 2
    lower_mask = jnp.tril(jnp.ones((half_size, half_size), jnp.float32))
    upper_mask = 1.0 - lower_mask
    corner = own_terms[half_size:, :half_size]
    packed = (
        own_terms[:half_size, :half_size] * lower_mask
        + own_terms[half_size:, half_size:] * upper_mask
    )
    second_diag = jnp.diagonal(own_terms[half_size:, half_size:])
    corner, packed, second_diag = packed_total(
        (corner, packed, second_diag), (("rows", "sub_0"), "sub_1")
    )
    strict_lower = jnp.tril(packed, -1)
    first_block = strict_lower + strict_lower.T + jnp.diag(jnp.diagonal(packed))
    strict_upper = packed * upper_mask
    second_block = strict_upper + strict_upper.T + jnp.diag(second_diag)
    top_rows = jnp.concatenate((first_block, corner.T), axis=1)
    bottom_rows = jnp.concatenate((corner, second_block), axis=1)
    gram_matrix = jnp.concatenate((top_rows, bottom_rows), axis=0)
    return jnp.linalg.cholesky(gram_matrix)


def solution(mesh):
    torus = Mesh(
        mesh.devices.reshape(mesh.shape["groups"], mesh.shape["rows"], 4, 2),
        ("groups", "rows", "sub_0", "sub_1"),
    )
    in_specs = (P(GROUPS_ROWS_SUB, None), P(GROUPS_ROWS_SUB), P("groups"))
    out_specs = P("groups", None)
    return jax.shard_map(body, mesh=torus, in_specs=in_specs, out_specs=out_specs, check_vma=False)
```

profile of v0, /device:TPU:33, one launch (start us, length us, event | category | flops | bytes accessed | tf_op | source)
XLA Modules:
  0.0 565.3 jit_solution(17192161763873769180)
XLA Ops:
  0.7 1.8 broadcast_multiply_fusion
  2.5 3.5 convolution_bitcast_fusion
  6.0 2.0 copy.58
  8.0 5.4 fusion.66
  13.3 1.2 copy.59
  14.6 1.6 reshape_reshape.9
  16.2 31.2 %all-to-all-start = ((f32[128,4,1024]{2,1,0:T(4,128)}), f32[128,4,1024]{2,1,0:T(4,128)S(1)}, u32[]{:S(2)}, u32[]{:S(2)}) async-start(f32[128,4,1024]{2,1,0:T(4,128)} %reshape_reshape.9), calls=%async_computation | async-start | bytes 4194304 | tf_op jit(solution)/shard_map/all_to_all | solution.py:107
  48.9 93.9 %all-to-all-done = f32[128,4,1024]{2,1,0:T(4,128)S(1)} async-done(((f32[128,4,1024]{2,1,0:T(4,128)}), f32[128,4,1024]{2,1,0:T(4,128)S(1)}, u32[]{:S(2)}, u32[]{:S(2)}) %all-to-all-start) | async-done | bytes 2097184 | tf_op jit(solution)/shard_map/all_to_all | solution.py:107
  142.7 3.0 fusion.5
  145.8 7.6 %bitcast_multiply_fusion = f32[1024,1024]{1,0:T(8,128)S(1)} fusion(f32[128,4,1024]{2,0,1:T(8,128)S(1)} %fusion.5, f32[128,4]{0,1:T(4,128)S(1)} %copy.61), kind=kOutput, calls=%fused_computation.6 | convolution fusion | flops 6444023808 | bytes 6293504 | tf_op jit(solution)/shard_map/rn,rm->nm/dot_general | solution.py:115
  154.7 4.5 gather_fusion
  159.3 1.5 pad_maximum_fusion
  160.7 3.7 reshape_reshape.10
  164.6 7.8 %all_to_all.30 = f32[2,64,4100]{2,1,0:T(8,128)S(1)} all-to-all(f32[2,64,4100]{2,1,0:T(8,128)S(1)} %copy.64), channel_id=1, replica_groups=mesh['groups'=2,'rows'=16,'sub_0'=4,'sub_1'=2] {'sub_1'}, dimensions={0} | all-to-all | bytes 4198400 | tf_op jit(solution)/shard_map/all_to_all | solution.py:46
  173.4 62.6 %all_to_all.31 = f32[64,1,4100]{2,1,0:T(1,128)S(1)} all-to-all(f32[64,1,4100]{2,1,0:T(1,128)S(1)} %all_to_all.21), channel_id=1, replica_groups=mesh['groups'=2,'rows'=16,'sub_0'=4,'sub_1'=2] {'rows','sub_0'}, dimensions={0} | all-to-all | bytes 2099200 | tf_op jit(solution)/shard_map/all_to_all | solution.py:53
  236.7 1.5 broadcast_in_dim.63
  238.3 8.1 %all-to-all-start.3 = ((f32[64,1,4100]{2,1,0:T(1,128)}), f32[64,1,4100]{2,1,0:T(1,128)S(1)}, u32[]{:S(2)}, u32[]{:S(2)}) async-start(f32[64,1,4100]{2,1,0:T(1,128)} %broadcast_in_dim.63), calls=%async_computation.3 | async-start | bytes 2162688 | tf_op jit(solution)/shard_map/all_to_all | solution.py:21
  246.4 51.3 %all-to-all-done.3 = f32[64,1,4100]{2,1,0:T(1,128)S(1)} async-done(((f32[64,1,4100]{2,1,0:T(1,128)}), f32[64,1,4100]{2,1,0:T(1,128)S(1)}, u32[]{:S(2)}, u32[]{:S(2)}) %all-to-all-start.3) | async-done | bytes 1049632 | tf_op jit(solution)/shard_map/all_to_all | solution.py:21
  297.9 10.1 %all_to_all.32 = f32[2,64,4100]{2,1,0:T(8,128)S(1)} all-to-all(f32[2,64,4100]{2,1,0:T(8,128)S(1)} %broadcast_in_dim.65), channel_id=1, replica_groups=mesh['groups'=2,'rows'=16,'sub_0'=4,'sub_1'=2] {'sub_1'}, dimensions={0} | all-to-all | bytes 4198400 | tf_op jit(solution)/shard_map/all_to_all | solution.py:21
  308.0 1.7 copy.65
  309.7 3.1 reshape_reshape.11
  312.8 3.6 slice.203
  316.4 1.5 fusion.7
  317.9 1.3 copy.69
  319.3 3.4 fusion.91
  322.7 8.9 %gather_fusion.1 = f32[512]{0:T(512)S(1)} fusion(f32[512,512]{1,0:T(8,128)} %get-tuple-element.8, s32[512]{0:T(512)S(1)} %bitcast.76), kind=kCustom, calls=%fused_computation.1 | custom fusion | bytes 8192 | tf_op jit(solution)/shard_map/jit(diagonal)/cond/branch_0_fun/gather | solution.py:131
  331.6 2.5 copy.72
  334.1 1.3 copy.71
  335.4 1.4 copy.67
  336.8 1.5 bitcast_add_fusion.2
  338.3 1.4 copy.68
  339.7 1.8 select_add_fusion
  341.5 3.7 maximum_maximum_fusion
  345.2 5.5 copy.73
  350.8 3.5 fusion
  354.2 1.9 copy-done.1
  356.2 11.7 %cholesky.223 = f32[128,128]{1,0:T(8,128)S(1)} custom-call(f32[128,128]{1,0:T(8,128)S(1)} %cholesky.580), custom_call_target="Cholesky" | custom-call | tf_op jit(solution)/shard_map/jit(cholesky)/cholesky | solution.py:137
  367.9 2.5 cholesky.255
  371.1 9.8 %custom-call.59 = f32[1,128,128]{1,2,0:T(8,128)S(1)} custom-call(f32[1,128,128]{2,1,0:T(8,128)S(1)} %get-tuple-element.34), custom_call_target="InvertDiagBlocksLowerTriangular" | custom-call | tf_op jit(solution)/shard_map/jit(cholesky)/cholesky | solution.py:137
  380.9 2.3 constant_dynamic-update-slice_fusion.5
  383.2 1.5 convolution_subtract_fusion
  384.8 12.1 %cholesky.244 = f32[128,128]{1,0:T(8,128)S(1)} custom-call(f32[128,128]{1,0:T(8,128)S(1)} %cholesky.584), custom_call_target="Cholesky" | custom-call | tf_op jit(solution)/shard_map/jit(cholesky)/cholesky | solution.py:137
  398.2 9.8 %custom-call.60 = f32[1,128,128]{1,2,0:T(8,128)S(1)} custom-call(f32[1,128,128]{2,1,0:T(8,128)S(1)} %get-tuple-element.31), custom_call_target="InvertDiagBlocksLowerTriangular" | custom-call | tf_op jit(solution)/shard_map/jit(cholesky)/cholesky | solution.py:137
  408.0 1.2 convolution_dynamic-update-slice_fusion
  409.2 2.1 convolution_subtract_fusion.1
  411.3 11.7 %cholesky.468 = f32[128,128]{1,0:T(8,128)S(1)} custom-call(f32[128,128]{1,0:T(8,128)S(1)} %cholesky.589), custom_call_target="Cholesky" | custom-call | tf_op jit(solution)/shard_map/jit(cholesky)/cholesky | solution.py:137
  424.4 9.8 %custom-call.61 = f32[1,128,128]{1,2,0:T(8,128)S(1)} custom-call(f32[1,128,128]{2,1,0:T(8,128)S(1)} %get-tuple-element.28), custom_call_target="InvertDiagBlocksLowerTriangular" | custom-call | tf_op jit(solution)/shard_map/jit(cholesky)/cholesky | solution.py:137
  434.2 1.1 convolution_dynamic-update-slice_fusion.1
  435.3 2.3 convolution_subtract_fusion.2
  437.7 11.9 %cholesky.487 = f32[128,128]{1,0:T(8,128)S(1)} custom-call(f32[128,128]{1,0:T(8,128)S(1)} %cholesky.594), custom_call_target="Cholesky" | custom-call | tf_op jit(solution)/shard_map/jit(cholesky)/cholesky | solution.py:137
  450.8 9.8 %custom-call.62 = f32[1,128,128]{1,2,0:T(8,128)S(1)} custom-call(f32[1,128,128]{2,1,0:T(8,128)S(1)} %get-tuple-element.25), custom_call_target="InvertDiagBlocksLowerTriangular" | custom-call | tf_op jit(solution)/shard_map/jit(cholesky)/cholesky | solution.py:137
  460.7 1.1 convolution_dynamic-update-slice_fusion.2
  461.7 2.4 convolution_subtract_fusion.3
  464.1 11.7 %cholesky.506 = f32[128,128]{1,0:T(8,128)S(1)} custom-call(f32[128,128]{1,0:T(8,128)S(1)} %cholesky.599), custom_call_target="Cholesky" | custom-call | tf_op jit(solution)/shard_map/jit(cholesky)/cholesky | solution.py:137
  477.1 10.0 %custom-call.63 = f32[1,128,128]{1,2,0:T(8,128)S(1)} custom-call(f32[1,128,128]{2,1,0:T(8,128)S(1)} %get-tuple-element.22), custom_call_target="InvertDiagBlocksLowerTriangular" | custom-call | tf_op jit(solution)/shard_map/jit(cholesky)/cholesky | solution.py:137
  488.1 2.3 convolution_subtract_fusion.4
  490.4 11.7 %cholesky.526 = f32[128,128]{1,0:T(8,128)S(1)} custom-call(f32[128,128]{1,0:T(8,128)S(1)} %cholesky.604), custom_call_target="Cholesky" | custom-call | tf_op jit(solution)/shard_map/jit(cholesky)/cholesky | solution.py:137
  503.4 9.8 %custom-call.64 = f32[1,128,128]{1,2,0:T(8,128)S(1)} custom-call(f32[1,128,128]{2,1,0:T(8,128)S(1)} %get-tuple-element.19), custom_call_target="InvertDiagBlocksLowerTriangular" | custom-call | tf_op jit(solution)/shard_map/jit(cholesky)/cholesky | solution.py:137
  514.2 2.0 convolution_subtract_fusion.5
  516.2 11.9 %cholesky.546 = f32[128,128]{1,0:T(8,128)S(1)} custom-call(f32[128,128]{1,0:T(8,128)S(1)} %cholesky.609), custom_call_target="Cholesky" | custom-call | tf_op jit(solution)/shard_map/jit(cholesky)/cholesky | solution.py:137
  529.5 9.8 %custom-call.65 = f32[1,128,128]{1,2,0:T(8,128)S(1)} custom-call(f32[1,128,128]{2,1,0:T(8,128)S(1)} %get-tuple-element.16), custom_call_target="InvertDiagBlocksLowerTriangular" | custom-call | tf_op jit(solution)/shard_map/jit(cholesky)/cholesky | solution.py:137
  540.1 1.8 convolution_subtract_fusion.6
  541.9 11.7 %cholesky.564 = f32[128,128]{1,0:T(8,128)S(1)} custom-call(f32[128,128]{1,0:T(8,128)S(1)} %convolution_subtract_fusion.6), custom_call_target="Cholesky" | custom-call | tf_op jit(solution)/shard_map/jit(cholesky)/cholesky | solution.py:137
  560.0 4.9 select_select_fusion
  (55 shorter events, 18.2 us)
Async XLA Ops:
  14.6 33.1 %copy-start.4 = (s32[4096]{0:T(1024)S(1)}, s32[4096]{0:T(1024)}, u32[]{:S(2)}) copy-start(s32[4096]{0:T(1024)} %param.5) | copy-start | bytes 49156
  16.2 126.5 %all-to-all-start = ((f32[128,4,1024]{2,1,0:T(4,128)}), f32[128,4,1024]{2,1,0:T(4,128)S(1)}, u32[]{:S(2)}, u32[]{:S(2)}) async-start(f32[128,4,1024]{2,1,0:T(4,128)} %reshape_reshape.9), calls=%async_computation | async-start | bytes 4194304 | tf_op jit(solution)/shard_map/all_to_all | solution.py:107
  238.3 59.4 %all-to-all-start.3 = ((f32[64,1,4100]{2,1,0:T(1,128)}), f32[64,1,4100]{2,1,0:T(1,128)S(1)}, u32[]{:S(2)}, u32[]{:S(2)}) async-start(f32[64,1,4100]{2,1,0:T(1,128)} %broadcast_in_dim.63), calls=%async_computation.3 | async-start | bytes 2162688 | tf_op jit(solution)/shard_map/all_to_all | solution.py:21
  316.4 2.8 copy-start
  322.7 11.4 %copy-start.3 = (f32[512,512]{1,0:T(8,128)S(1)}, f32[512,512]{1,0:T(8,128)}, u32[]{:S(2)}) copy-start(f32[512,512]{1,0:T(8,128)} %get-tuple-element.9) | copy-start | bytes 3145732
  335.4 4.2 slice-start
  336.8 4.7 copy-start.2
  354.2 1.9 copy-start.1
where the time goes:
time: 576 us; the launch traced here: 565 us
  other arithmetic  200 us (35%)
  waiting for transfers between devices  145 us (25%)
  blocking collectives  80.5 us (14%)
  local copies, waits for them, and re-layouts  52.1 us (9%)
  matrix products  42.5 us (7%)
  starting transfers between devices  39.3 us (7%)
  between operations  5.88 us (1%)
    another operation x31, other arithmetic, body(): return jnp.linalg.cholesky(gram_matrix)  173 us
    all_to_all x1, waiting for transfers between devices, body(): lax.all_to_all(blocks, ROWS_SUB, split_axis=0, concat_axis=0, tiled=True)  93.9 us
    all_to_all x1, blocking collectives, sum_by_axis(): return jnp.sum(lax.all_to_all(own, far, 0, 0, tiled=True), axis=0)  62.6 us
    all_to_all x1, waiting for transfers between devices, from_everyone(): lax.all_to_all(jnp.broadcast_to(array[None], (peers, *array.shape)), axis...  51.3 us
    all_to_all x1, starting transfers between devices, body(): lax.all_to_all(blocks, ROWS_SUB, split_axis=0, concat_axis=0, tiled=True)  31.2 us
    another operation x14, matrix products, body(): return jnp.linalg.cholesky(gram_matrix)  22.9 us
  transfers between devices with their start and end apart: 2, of which 2 were waited for; matrix products, arithmetic and copies ran while one was open for 0% of the time, Pallas kernels for 0%

commit v1 on v0

v1 whole, which is shorter than its diff:
```python
import functools

import jax
import jax.numpy as jnp
from jax import lax
from jax.experimental import pallas as pl
from jax.experimental.pallas import tpu as pltpu
from jax.sharding import Mesh
from jax.sharding import PartitionSpec as P

GROUPS_ROWS_SUB = ("groups", "rows", "sub_0", "sub_1")
BLK = 128
SUB = 32
SUB0 = 4
SLOTS = 5
PIECES = 2
F32 = jnp.float32
BF = jnp.bfloat16


def row_of(vec, s):
    return jnp.broadcast_to(vec[s:s + 1, :], vec.shape)


def split(x):
    hi = x.astype(BF)
    return hi, (x - hi.astype(F32)).astype(BF)


def dot3(ah, al, bh, bl):
    d = functools.partial(jnp.dot, preferred_element_type=F32)
    return d(ah, bh) + (d(ah, bl) + d(al, bh))


def factor_diagonal(w, u):
    for p in range(BLK // SUB):
        r0 = SUB * p
        ngrp = SUB // 8
        sl = [slice(r0 + 8 * g, r0 + 8 * g + 8) for g in range(ngrp)]
        ta = [w[sl[g], 0:BLK] for g in range(ngrp)]
        te = [w[sl[g], BLK:2 * BLK] for g in range(ngrp)]
        cols = {}
        for c in range(SUB):
            for g in range(c // 8, ngrp):
                cols[c, g] = jnp.broadcast_to(ta[g][:, r0 + c:r0 + c + 1], (8, BLK))
        for i in range(SUB):
            g, s = divmod(i, 8)
            r = lax.rsqrt(row_of(cols[i, g], s))
            lo = {h: cols[i, h] * r for h in range(g, ngrp)}
            ua = row_of(ta[g], s) * r
            ue = row_of(te[g], s) * r
            u[r0 + i:r0 + i + 1, 0:BLK] = ua[0:1]
            u[r0 + i:r0 + i + 1, BLK:2 * BLK] = ue[0:1]
            for c in range(i + 1, SUB):
                m = row_of(lo[c // 8], c % 8)
                for h in range(c // 8, ngrp):
                    cols[c, h] = cols[c, h] - lo[h] * m
            for h in range(g, ngrp):
                if h > g or s < 7:
                    ta[h] = ta[h] - lo[h] * ua
                    te[h] = te[h] - lo[h] * ue
        if p + 1 < BLK // SUB:
            n0 = r0 + SUB
            hi, lw = split(u[r0:n0, :])
            left = jnp.concatenate([hi, hi, lw, lw], axis=0)[:, 0:BLK]
            right = jnp.concatenate([hi, lw, hi, lw], axis=0)
            upd = lax.dot_general(left, right, (((0,), (0,)), ((), ())), preferred_element_type=F32)
            w[n0:BLK, :] = w[n0:BLK, :] - upd[n0:BLK, :]


def chol_kernel(nb, a_ref, l_ref, w, pw, u, uh, ul, lh, ll):
    ii = lax.broadcasted_iota(jnp.int32, (BLK, BLK), 0)
    jj = lax.broadcasted_iota(jnp.int32, (BLK, BLK), 1)
    eye = jnp.where(ii == jj, 1.0, 0.0).astype(F32)

    where = gram_places()

    def step(k, carry):
        for q in range(nb):
            @pl.when(k == q)
            def _(q=q):
                c0 = q * BLK
                width = (nb - q) * BLK
                if q:
                    s = dot3(lh[c0:c0 + BLK, 0:c0], ll[c0:c0 + BLK, 0:c0], uh[0:c0, c0:], ul[0:c0, c0:])
                for j in range(q, nb):
                    owner, slot = where[q, j]
                    blk = a_ref[owner, slot * BLK:(slot + 1) * BLK, :]
                    if q:
                        o = (j - q) * BLK
                        blk = blk - s[:, o:o + BLK]
                    if j == q:
                        w[:, 0:BLK] = blk
                    else:
                        pw[:, (j - 1) * BLK:j * BLK] = blk
        w[:, BLK:2 * BLK] = eye
        factor_diagonal(w, u)
        for q in range(nb):
            @pl.when(k == q)
            def _(q=q):
                c0 = q * BLK
                l_ref[c0:c0 + BLK, c0:c0 + BLK] = jnp.where(ii <= jj, u[:, 0:BLK], 0.0).T
                for j in range(q + 1, nb):
                    l_ref[c0:c0 + BLK, j * BLK:(j + 1) * BLK] = jnp.zeros((BLK, BLK), F32)
                if q + 1 < nb:
                    ih, il = split(u[:, BLK:2 * BLK])
                    ph, plo = split(pw[:, c0:])
                    res = dot3(ih, il, ph, plo)
                    rh, rl = split(res)
                    uh[c0:c0 + BLK, c0 + BLK:] = rh
                    ul[c0:c0 + BLK, c0 + BLK:] = rl
                    for j in range(q + 1, nb):
                        o = (j - q - 1) * BLK
                        t = res[:, o:o + BLK].T
                        l_ref[j * BLK:(j + 1) * BLK, c0:c0 + BLK] = t
                        th, tl = split(t)
                        lh[j * BLK:(j + 1) * BLK, c0:c0 + BLK] = th
                        ll[j * BLK:(j + 1) * BLK, c0:c0 + BLK] = tl
        return carry

    lax.fori_loop(0, nb, step, 0)


def cholesky_blocks(a, n):
    nb = n // BLK
    return pl.pallas_call(
        functools.partial(chol_kernel, nb),
        out_shape=jax.ShapeDtypeStruct((n, n), F32),
        in_specs=[pl.BlockSpec(memory_space=pltpu.VMEM)],
        out_specs=pl.BlockSpec(memory_space=pltpu.VMEM),
        scratch_shapes=[
            pltpu.VMEM((BLK, 2 * BLK), F32),
            pltpu.VMEM((BLK, n - BLK), F32),
            pltpu.VMEM((BLK, 2 * BLK), F32),
            pltpu.VMEM((n, n), BF), pltpu.VMEM((n, n), BF),
            pltpu.VMEM((n, n), BF), pltpu.VMEM((n, n), BF),
        ],
        compiler_params=pltpu.CompilerParams(vmem_limit_bytes=40 * 2**20),
        name="block_cholesky",
    )(a)


def wrap(v, n):
    return lax.rem(v + n, n)


def hadamard_signs(rows, columns):
    both = jnp.bitwise_and(
        lax.broadcasted_iota(jnp.int32, (rows, columns), 0),
        lax.broadcasted_iota(jnp.int32, (rows, columns), 1),
    )
    shift = 8
    while shift:
        both = jnp.bitwise_xor(both, jnp.right_shift(both, shift))
        shift //= 2
    return (1 - 2 * jnp.bitwise_and(both, 1)).astype(F32)


def place():
    z, x, c = (lax.axis_index(a) for a in ("rows", "sub_0", "sub_1"))
    return z, x, c, 2 * x + c


def remote(src, dst, send, recv, **where):
    return pltpu.make_async_remote_copy(
        src_ref=src, dst_ref=dst, send_sem=send, recv_sem=recv,
        device_id=where, device_id_type=pl.DeviceIdType.MESH,
    )


def signal(sem, **where):
    pl.semaphore_signal(sem, inc=1, device_id=where, device_id_type=pl.DeviceIdType.MESH)


def sub_step(k, x, c):
    far = jnp.bitwise_xor(k // 2, k // 4)
    return wrap(x + far, SUB0), wrap(x - far, SUB0), lax.rem(c + lax.rem(k, 2), 2)


def exchange_and_mix(x_ref, sg_ref, recv, sgall, hmat, tab, own_sem, sends, recvs, sgs, sgr):
    z, x, c, s_me = place()
    rows = x_ref.shape[0]

    def column(s):
        return x_ref.at[:, pl.ds(pl.multiple_of(s * BLK, BLK), BLK)]

    def data(k):
        to, src, core = sub_step(k, x, c)
        return remote(column(2 * to + core), recv.at[s_me], sends.at[k], recvs.at[k],
                      sub_0=to, sub_1=core), 2 * src + core

    def signs(k):
        to, src, core = sub_step(k, x, c)
        return remote(sg_ref, sgall.at[s_me], sgs.at[k], sgr.at[k], sub_0=to, sub_1=core)

    def start(k, carry):
        signs(k).start()
        data(k)[0].start()
        return carry

    own = pltpu.make_async_copy(column(s_me), recv.at[s_me], own_sem)
    own.start()
    lax.fori_loop(1, 8, start, 0)
    sgall[s_me] = sg_ref[...]
    base = hadamard_signs(BLK, BLK)
    for a in range(rows // BLK):
        for b in range(rows // BLK):
            sign = -1.0 if bin(a & b).count("1") % 2 else 1.0
            hmat[a * BLK:(a + 1) * BLK, b * BLK:(b + 1) * BLK] = (base * sign).astype(BF)

    def transform(s):
        left = hmat[...] * sgall[s].astype(BF)
        hi, lo = split(recv[s])
        both = jnp.concatenate([hi, lo], axis=1)
        res = jnp.dot(left, both, preferred_element_type=F32)
        tab[pl.ds(pl.multiple_of(s * rows, rows), rows), :] = res[:, :BLK] + res[:, BLK:]

    own.wait()
    transform(s_me)

    def arrive(k, carry):
        copy, s = data(k)
        signs(k).wait_recv()
        copy.wait_recv()
        transform(s)
        return carry

    lax.fori_loop(1, 8, arrive, 0)

    def mix(q, carry):
        at = [pl.ds(pl.multiple_of(s * rows + 8 * q, 8), 8) for s in range(8)]
        v = [tab[at[s], :] for s in range(8)]
        for bit in (1, 2, 4):
            v = [v[s ^ bit] - v[s] if s & bit else v[s] + v[s ^ bit] for s in range(8)]
        for s in range(8):
            w = v[s] * (1.0 / 256.0)
            tab[at[s], :] = w
            tab[pl.ds(pl.multiple_of((8 + s) * rows + 8 * q, 8), 8), :] = -w
        return carry

    lax.fori_loop(0, rows // 8, mix, 0)

    def finish(k, carry):
        data(k)[0].wait_send()
        signs(k).wait_send()
        return carry

    lax.fori_loop(1, 8, finish, 0)


def ring_sum(length, pieces, own_term, last, bufs, sems):
    z, x, c, s_me = place()
    up = 1 - 2 * c
    send_buf, recv_buf = bufs
    sent, got = sems
    half = length // 2

    def copy(w, t, h):
        to = wrap(z + up * (1 - 2 * w), length)
        return remote(send_buf.at[w, t, h], recv_buf.at[w, t, h],
                      sent.at[w, t, h], got.at[w, t, h], rows=to)

    def dest(w, t):
        return wrap(z + up * (1 - 2 * w) * (half - w - t), length)

    for h in range(pieces):
        for w in range(2):
            own_term(dest(w, 0), h, send_buf.at[w, 0, h])
            copy(w, 0, h).start()

    def advance(w, t):
        for h in range(pieces):
            own_term(dest(w, t), h, send_buf.at[w, t, h])
        for h in range(pieces):
            copy(w, t - 1, h).wait_recv()
            send_buf[w, t, h] = send_buf[w, t, h] + recv_buf[w, t - 1, h]
            copy(w, t, h).start()

    def step(t, carry):
        advance(0, t)
        advance(1, t)
        return carry

    lax.fori_loop(1, half - 1, step, 0)
    advance(0, half - 1)
    for h in range(pieces):
        own_term(z, h, last.at[h])
    for h in range(pieces):
        copy(1, half - 2, h).wait_recv()
        last[h] = last[h] + recv_buf[1, half - 2, h]
        copy(0, half - 1, h).wait_recv()
        last[h] = last[h] + recv_buf[0, half - 1, h]

    def finish(t, carry):
        for w in range(2):
            for h in range(pieces):
                copy(w, t, h).wait_send()
        return carry

    lax.fori_loop(0, half - 1, finish, 0)
    for h in range(pieces):
        copy(0, half - 1, h).wait_send()


def ring_gather(length, rows, buf, sems):
    z, x, c, s_me = place()
    up = 1 - 2 * c
    sent, got = sems
    half = length // 2

    def copy(w, t):
        way = up * (1 - 2 * w)
        piece = wrap(z - way * t, length)
        part = buf.at[pl.ds(pl.multiple_of(piece * rows, 8), rows), :]
        return remote(part, part, sent.at[w, t], got.at[w, t], rows=wrap(z + way, length))

    def arrived(w, t):
        way = up * (1 - 2 * w)
        piece = wrap(z - way * (t + 1), length)
        part = buf.at[pl.ds(pl.multiple_of(piece * rows, 8), rows), :]
        remote(part, part, sent.at[w, t], got.at[w, t], rows=wrap(z + way, length)).wait_recv()

    copy(0, 0).start()
    copy(1, 0).start()

    def step(t, carry):
        for w in range(2):
            arrived(w, t - 1)
            copy(w, t).start()
        return carry

    lax.fori_loop(1, half - 1, step, 0)
    arrived(0, half - 2)
    copy(0, half - 1).start()
    arrived(1, half - 2)
    arrived(0, half - 1)

    def finish(t, carry):
        for w in range(2):
            copy(w, t).wait_send()
        return carry

    lax.fori_loop(0, half - 1, finish, 0)
    copy(0, half - 1).wait_send()


def gram_pair(slot, x, c):
    s = 2 * x + c
    right, left = 2 * ((x + 1) % SUB0), 2 * ((x + SUB0 - 1) % SUB0)
    return [
        (s, s), (s, right), (s, right + 1),
        (left + c, right + (c + x // 2) % 2),
        (2 * x, 2 * x + 1),
    ][slot]


def gram_places():
    where = {}
    for x in range(SUB0):
        for c in range(2):
            for slot in range(SLOTS):
                a, b = gram_pair(slot, x, c)
                where.setdefault((min(a, b), max(a, b)), (2 * x + c, slot))
    return where


def share_picks(picks, sems):
    z, x, c, s_me = place()
    sent, got = sems
    steps = [(0, 1), (1, 0), (1, 1), (3, 0), (3, 1)]
    copies = []
    for k, (far, flip) in enumerate(steps):
        to, core = wrap(x + far, SUB0), lax.rem(c + flip, 2)
        cp = remote(picks.at[s_me], picks.at[s_me], sent.at[k], got.at[k], sub_0=to, sub_1=core)
        cp.start()
    for k, (far, flip) in enumerate(steps):
        src, core = 2 * wrap(x - far, SUB0) + lax.rem(c + flip, 2), lax.rem(c + flip, 2)
        cp = remote(picks.at[src], picks.at[src], sent.at[k], got.at[k],
                    sub_0=wrap(x + far, SUB0), sub_1=core)
        copies.append(cp)
        cp.wait_recv()
    for cp in copies:
        cp.wait_send()


def gram_parts(picks, parts, scale):
    z, x, c, s_me = place()
    tdot = lambda a, b: lax.dot_general(a, b, (((0,), (0,)), ((), ())), preferred_element_type=F32)
    for slot in range(SLOTS):
        a, b = gram_pair(slot, x, c)
        ah, al = split(picks[jnp.minimum(a, b)])
        bh, bl = split(picks[jnp.maximum(a, b)])
        parts[slot * BLK:(slot + 1) * BLK, :] = (tdot(ah, bh) + (tdot(ah, bl) + tdot(al, bh))) * scale


def share_blocks(total, out_ref, sems):
    z, x, c, s_me = place()
    sent, got, dsent, dgot = sems
    rows = total.shape[0]
    half = rows // 2
    cut = [pl.ds(0, half), pl.ds(half, half)]
    left, right = wrap(x - 1, SUB0), wrap(x + 1, SUB0)
    across = wrap(x + 2, SUB0)

    def hop(way, k, owner, part):
        ref = out_ref.at[2 * owner + c, cut[part]]
        return remote(ref, ref, sent.at[way, k], got.at[way, k], sub_0=right if way == 0 else left)

    def over(k, owner, part):
        ref = out_ref.at[2 * owner + c, cut[part]]
        return remote(ref, ref, dsent.at[k], dgot.at[k], sub_1=1 - c)

    def came(k, owner, part):
        ref = out_ref.at[2 * owner + (1 - c), cut[part]]
        return remote(ref, ref, dsent.at[k], dgot.at[k], sub_1=1 - c)

    out_ref[s_me] = total[...]
    for way in range(2):
        hop(way, 0, x, way).start()
    for way in range(2):
        hop(way, 1, x, 1 - way).start()
    for part in range(2):
        over(part, x, part).start()
    back = [left, right]
    for way in range(2):
        hop(way, 0, back[way], way).wait_recv()
        hop(way, 2, back[way], way).start()
        over(2 + way, back[way], way).start()
    for way in range(2):
        hop(way, 1, back[way], 1 - way).wait_recv()
        over(4 + way, back[way], 1 - way).start()
    for way in range(2):
        hop(way, 2, across, way).wait_recv()
        over(6 + way, across, way).start()
    order = [(0, x, 0), (1, x, 1), (2, left, 0), (3, right, 1), (4, left, 1), (5, right, 0),
             (6, across, 0), (7, across, 1)]
    for k, owner, part in order:
        came(k, owner, part).wait_recv()
    for way in range(2):
        hop(way, 0, x, way).wait_send()
        hop(way, 1, x, 1 - way).wait_send()
        hop(way, 2, back[way], way).wait_send()
    for k, owner, part in order:
        over(k, owner, part).wait_send()


def sketch_kernel(length, scale, stop, x_ref, sg_ref, idx_ref, out_ref,
                  recv, sgall, hmat, tab, pbuf_s, pbuf_r, last, picks, parts, gbuf_s, gbuf_r,
                  glast, total, own_sem, a_s, a_r, g_s, g_r, p_s, p_r, q_s, q_r, e_s, e_r,
                  w_s, w_r, h_s, h_r, d_s, d_r):
    z, x, c, s_me = place()
    barrier = pltpu.get_barrier_semaphore()
    for k in range(1, 8):
        signal(barrier, sub_0=wrap(x + k // 2, SUB0), sub_1=lax.rem(c + k % 2, 2))
    for far in (1, length - 1):
        signal(barrier, rows=wrap(z + far, length))
    pl.semaphore_wait(barrier, 9)

    exchange_and_mix(x_ref, sg_ref, recv, sgall, hmat, tab, own_sem, a_s, a_r, g_s, g_r)
    pieces, rows = last.shape[0], last.shape[1]

    def gather(dest, part, ref):
        def some(q, carry):
            for e in range(8):
                j = idx_ref[dest, part * rows + 8 * q + e]
                ref[pl.ds(8 * q + e, 1), :] = tab[pl.ds(j, 1), :]
            return carry

        lax.fori_loop(0, rows // 8, some, 0)

    ring_sum(length, pieces, gather, last, (pbuf_s, pbuf_r), (p_s, p_r))
    for h in range(pieces):
        picks[s_me, h * rows:(h + 1) * rows, :] = last[h]
    share_picks(picks, (e_s, e_r))
    gram_parts(picks, parts, scale)
    small = glast.shape[1]

    def own_part(dest, part, ref):
        ref[...] = parts[pl.ds(pl.multiple_of(dest * small, 8), small), :]

    ring_sum(length, 1, own_part, glast, (gbuf_s, gbuf_r), (q_s, q_r))
    total[pl.ds(pl.multiple_of(z * small, 8), small), :] = glast[0]
    ring_gather(length, small, total, (w_s, w_r))
    share_blocks(total, out_ref, (h_s, h_r, d_s, d_r))


def sketch_gram(matrix, signs, index, scale):
    rows, columns = matrix.shape
    length, samples = index.shape
    half = length // 2
    pieces = PIECES
    small = SLOTS * BLK // length
    dma = pltpu.SemaphoreType.DMA
    return pl.pallas_call(
        functools.partial(sketch_kernel, length, scale, 0),
        out_shape=jax.ShapeDtypeStruct((columns // BLK, SLOTS * BLK, BLK), F32),
        in_specs=[
            pl.BlockSpec(memory_space=pl.ANY),
            pl.BlockSpec(memory_space=pltpu.VMEM),
            pl.BlockSpec(memory_space=pltpu.SMEM),
        ],
        out_specs=pl.BlockSpec(memory_space=pltpu.VMEM),
        scratch_shapes=[
            pltpu.VMEM((8, rows, BLK), F32), pltpu.VMEM((8, 1, rows), F32),
            pltpu.VMEM((rows, rows), BF), pltpu.VMEM((16 * rows, BLK), F32),
            pltpu.VMEM((2, half, pieces, samples // pieces, BLK), F32),
            pltpu.VMEM((2, half, pieces, samples // pieces, BLK), F32),
            pltpu.VMEM((pieces, samples // pieces, BLK), F32),
            pltpu.VMEM((8, samples, BLK), F32),
            pltpu.VMEM((SLOTS * BLK, BLK), F32),
            pltpu.VMEM((2, half, 1, small, BLK), F32), pltpu.VMEM((2, half, 1, small, BLK), F32),
            pltpu.VMEM((1, small, BLK), F32), pltpu.VMEM((SLOTS * BLK, BLK), F32),
            dma, dma((8,)), dma((8,)), dma((8,)), dma((8,)),
            dma((2, half, pieces)), dma((2, half, pieces)),
            dma((2, half, 1)), dma((2, half, 1)), dma((5,)), dma((5,)),
            dma((2, half)), dma((2, half)), dma((2, 3)), dma((2, 3)), dma((8,)), dma((8,)),
        ],
        compiler_params=pltpu.CompilerParams(
            collective_id=0, has_side_effects=True, vmem_limit_bytes=48 * 2**20),
        name="sketch_gram",
    )(matrix, signs, index)


def body(matrix, sign_bits, samples):
    rows, columns = matrix.shape
    length = lax.axis_size("rows")
    z = lax.axis_index("rows")
    signs = (2 * sign_bits - 1).astype(F32).reshape(1, rows)
    local = 8 * rows
    high = jnp.bitwise_and(samples // local, z)
    shift = 8
    while shift:
        high = jnp.bitwise_xor(high, jnp.right_shift(high, shift))
        shift //= 2
    index = samples % local + local * jnp.bitwise_and(high, 1)
    blocks = sketch_gram(matrix, signs, index.reshape(length, -1), 1.0 / samples.shape[0])
    return cholesky_blocks(blocks, columns)


def solution(mesh):
    torus = Mesh(
        mesh.devices.reshape(mesh.shape["groups"], mesh.shape["rows"], SUB0, 2),
        ("groups", "rows", "sub_0", "sub_1"),
    )
    in_specs = (P(GROUPS_ROWS_SUB, None), P(GROUPS_ROWS_SUB), P("groups"))
    return jax.shard_map(
        body, mesh=torus, in_specs=in_specs, out_specs=P("groups", None), check_vma=False)
```

time: 576 us -> 186 us (0.32); the launches traced: 565 us -> 186 us
  other arithmetic: 200 us -> 1.43 us
  Pallas kernels: 0 us -> 182 us
  waiting for transfers between devices: 145 us -> 0 us
  blocking collectives: 80.5 us -> 0 us
  local copies, waits for them, and re-layouts: 52.1 us -> 1.59 us
  matrix products: 42.5 us -> 0 us
  starting transfers between devices: 39.3 us -> 0 us
  between operations: 5.88 us -> 0.02 us
    pallas_call x0 -> x2, Pallas kernels: none -> 182 us  [the longest x1 151 us: sketch_gram(): pl.pallas_call(functools.partial(sketch_kernel, length, scale, 0), out_sh...]
    another operation x31 -> x0, other arithmetic: 173 us -> none  [body(): return jnp.linalg.cholesky(gram_matrix)]
    all_to_all x2 -> x0, waiting for transfers between devices: 145 us -> none  [the longest x1 93.9 us: body(): lax.all_to_all(blocks, ROWS_SUB, split_axis=0, concat_axis=0, tiled=True)]
    all_to_all x3 -> x0, blocking collectives: 80.5 us -> none  [the longest x1 62.6 us: sum_by_axis(): return jnp.sum(lax.all_to_all(own, far, 0, 0, tiled=True), axis=0)]
    all_to_all x2 -> x0, starting transfers between devices: 39.3 us -> none  [the longest x1 31.2 us: body(): lax.all_to_all(blocks, ROWS_SUB, split_axis=0, concat_axis=0, tiled=True)]
    another operation x14 -> x0, matrix products: 22.9 us -> none  [body(): return jnp.linalg.cholesky(gram_matrix)]
    dot_general x4 -> x0, matrix products: 19.5 us -> none  [the longest x1 7.63 us: body(): jnp.einsum('rn,rm->nm', weighted, owned_rows, precision=HIGHEST)]
    gather x2 -> x0, local copies, waits for them, and re-layouts: 13.4 us -> none  [the longest x1 8.87 us: body(): first_block = strict_lower + strict_lower.T + jnp.diag(jnp.diagonal(packed))]
  transfers between devices with their start and end apart: 2 -> 0, of which waited for: 2 -> 0; matrix products, arithmetic and copies ran while one was open for 0% -> 0% of each run, Pallas kernels for 0% -> 0%
where the time goes in v1:
time: 186 us
  Pallas kernels  182 us (98%)
    pallas_call x1, Pallas kernels, sketch_gram(): pl.pallas_call(functools.partial(sketch_kernel, length, scale, 0), out_sh...  151 us
    pallas_call x1, Pallas kernels, cholesky_blocks(): pl.pallas_call(functools.partial(chol_kernel, nb), out_shape=jax.ShapeDty...  31.4 us

profile of v1, /device:TPU:33, one launch (start us, length us, event | category | flops | bytes accessed | tf_op | source)
XLA Modules:
  0.0 185.5 jit_solution(11417588573643420570)
XLA Ops:
  0.0 0.7 add_convert_fusion
  0.7 0.7 fusion
  1.4 0.0 copy-start
  1.5 1.6 copy-done
  3.0 151.1 %sketch_gram.1.a_ref = f32[8,640,128]{2,1,0:T(8,128)S(1)} custom-call(f32[512,1024]{1,0:T(8,128)S(1)} %copy-done, f32[1,512]{1,0:T(1,128)S(1)} %bitcast.1, s32[16,256]{1,0:T(8,128)S(1)} %reshape.7.idx_ref), custom_call_target="tpu_custom_call" | custom-call | tf_op jit(solution)/shard_map/sketch_gram/pallas_call | solution.py:494
  154.1 31.4 %block_cholesky.1 = f32[1024,1024]{1,0:T(8,128)} custom-call(f32[8,640,128]{2,1,0:T(8,128)S(1)} %sketch_gram.1.a_ref), custom_call_target="tpu_custom_call" | custom-call | tf_op jit(solution)/shard_map/block_cholesky/pallas_call | solution.py:126
  (1 shorter events, 0.0 us)
Async XLA Ops:
  1.4 1.6 copy-start
